TPU v7x, 32 devices: a whole 2x2x4 slice. The times are simulated.
32 devices in a mesh: member: 4 (over y, core), space: 8 (over z, x).
Axes of the slice: x: 2, y: 2, z: 4, core: 2. Of those that a mesh axis runs over, the one named last changes fastest.
Arguments:
- state: float32 [256, 128, 1024], P('member', 'space'), may hold values from -8 to 8
- obs_index: int32 [8192], P('space'), may hold values from 0 to 16383
- obs_value: float32 [8192], P('space'), may hold values from -6 to 6
- obs_scale: float32 [8192], P('space'), may hold values from 0.3 to 3
- ksat: float32 [128, 1024], P('space'), may hold values from 0.05 to 0.2
- storage: float32 [128, 1024], P('space'), may hold values from 0.5 to 4
- recharge: float32 [128, 1024], P('space'), may hold values from -1.8 to 1.8
- newton_counts: int32 [256], replicated, may hold values from 1 to 8, as said below
Outputs:
- forecast: float32 [256, 128, 1024], P('member', 'space')
Inputs may be any that keep to these rules, and one draw needn't show every extreme that they name: `newton_counts`: A count of 8 occurs in every draw.
All inputs are finite; a program needn't handle non-finite values.
Results may differ from a plain program's by a relative error of at most 0.0003.
Values sent between devices are 32-bit elements; how exact they have to be, the bound alone decides.
A program may use at most 64 MiB of HBM per device.

v0:
```python
import jax
import jax.numpy as jnp
from jax import lax
from jax.sharding import PartitionSpec as P

KMAX = 8
NS_ITERS = 12
HIGHEST_PRECISION = lax.Precision.HIGHEST
DAMPING = 0.3


def padded_2(array, sides, width):
    for axis, dim in sides:
        peers, length = (lax.axis_size(axis), array.shape[dim])
        up = [(i, (i + 1) % peers) for i in range(peers - 1)]
        down = [(j, i) for i, j in up]
        last = lax.slice_in_dim(array, length - width, length, axis=dim)
        leading = lax.slice_in_dim(array, 0, width, axis=dim)
        before = lax.ppermute(last, axis, up)
        after = lax.ppermute(leading, axis, down)
        array = jnp.concatenate([before, array, after], axis=dim)
    return array


def inverse_root(gram_matrix):
    order_size = gram_matrix.shape[0]
    identity = jnp.eye(order_size, dtype=jnp.float32)
    whole = identity + gram_matrix
    norm_value = jnp.sqrt(jnp.sum(whole * whole))
    upper_iter = whole / norm_value
    lower_iter = identity
    for sweep_index in range(NS_ITERS):
        middle = 1.5 * identity - 0.5 * jnp.dot(lower_iter, upper_iter, precision=HIGHEST_PRECISION)
        upper_iter = jnp.dot(upper_iter, middle, precision=HIGHEST_PRECISION)
        lower_iter = jnp.dot(middle, lower_iter, precision=HIGHEST_PRECISION)
    return lower_iter / jnp.sqrt(norm_value)


def face_flux(padded, conduct):
    wide_level = jnp.pad(padded, ((0, 0), (0, 0), (1, 1)))
    wide_cond = jnp.pad(conduct, ((0, 0), (0, 0), (1, 1)))
    centre_level = wide_level[:, 1:-1, 1:-1]
    centre_cond = wide_cond[:, 1:-1, 1:-1]
    height = centre_level.shape[1]
    breadth = centre_level.shape[2]
    divergence = jnp.zeros_like(centre_level)
    for offset_row, offset_col in ((0, 1), (2, 1), (1, 0), (1, 2)):
        other_level = wide_level[
            :, offset_row : offset_row + height, offset_col : offset_col + breadth
        ]
        other_cond = wide_cond[
            :, offset_row : offset_row + height, offset_col : offset_col + breadth
        ]
        divergence = divergence + 0.5 * (centre_cond + other_cond) * (other_level - centre_level)
    return divergence


def sweep_group(start_iter, goal, storage, group_counts):

    def sweep_once(sweep_index, iterate):
        bend_value = jnp.tanh(iterate)
        derivative = 1.0 + storage * (1.0 - bend_value * bend_value)
        stepped = iterate - DAMPING * (iterate + storage * bend_value - goal) / derivative
        return jnp.where((group_counts > sweep_index)[:, None, None], stepped, iterate)

    return lax.fori_loop(0, jnp.max(group_counts), sweep_once, start_iter)


def relax(pressure, drive_term, storage, counts):
    target = pressure + storage * jnp.tanh(pressure) + drive_term
    pieces = []
    for first_member in range(0, pressure.shape[0], 8):
        pieces.append(
            sweep_group(
                pressure[first_member : first_member + 8],
                target[first_member : first_member + 8],
                storage,
                counts[first_member : first_member + 8],
            )
        )
    return jnp.concatenate(pieces, axis=0)


def advance(padded, padded_ksat, storage, recharge, counts):
    conduct = padded_ksat * jax.nn.sigmoid(padded)
    drive_term = face_flux(padded, conduct) + recharge
    return relax(padded[:, 1:-1], drive_term, storage, counts)


def on_device(state, obs_index, obs_value, obs_scale, ksat, storage, recharge, newton_counts):
    local_members, tile_rows, tile_width = state.shape
    groups = lax.axis_size("member")
    members = local_members * groups
    tile_cells = tile_rows * tile_width
    block_cells = tile_cells // groups
    share = local_members // groups
    position = lax.axis_index("member")
    regrouped = lax.all_to_all(
        state.reshape(local_members, tile_cells), "member", split_axis=1, concat_axis=0, tiled=True
    )
    mean_state = jnp.mean(regrouped, axis=0)
    anomaly = regrouped - mean_state
    local_cell = obs_index - position * block_cells
    inside = (local_cell >= 0) & (local_cell < block_cells)
    picked = jnp.clip(local_cell, 0, block_cells - 1)
    weight = jnp.where(inside, obs_scale, 0.0)
    root_count = jnp.sqrt(jnp.float32(members - 1))
    spread = jnp.take(anomaly, picked, axis=1) * weight / root_count
    innovation = weight * (obs_value - jnp.take(mean_state, picked))
    gram_part = jnp.dot(spread, spread.T, precision=HIGHEST_PRECISION)
    drive_part = jnp.dot(spread, innovation, precision=HIGHEST_PRECISION)
    gram_matrix, drive_vector = lax.psum((gram_part, drive_part), ("member", "space"))
    root_inverse = inverse_root(gram_matrix)
    mean_weights = jnp.dot(
        root_inverse,
        jnp.dot(root_inverse, drive_vector, precision=HIGHEST_PRECISION),
        precision=HIGHEST_PRECISION,
    )
    transform = mean_weights[:, None] / root_count + root_inverse
    sequence = jnp.arange(members, dtype=jnp.int32)
    owner_of = sequence // local_members
    sort_key = owner_of * ((KMAX + 1) * members) + (KMAX - newton_counts) * members + sequence
    ranking = jnp.argsort(sort_key)
    member_ids = ranking.reshape(groups, share, groups).transpose(2, 0, 1).reshape(members)
    transform = jnp.take(transform, member_ids, axis=1)
    own_ids = lax.dynamic_slice_in_dim(member_ids, position * local_members, local_members)
    own_counts = jnp.take(newton_counts, own_ids)
    analysis = mean_state + jnp.dot(transform.T, anomaly, precision=HIGHEST_PRECISION)
    owned = lax.all_to_all(analysis, "member", split_axis=0, concat_axis=1, tiled=True)
    pressure = owned.reshape(local_members, tile_rows, tile_width)
    stacked = jnp.concatenate([pressure, ksat[None]], axis=0)
    widened = padded_2(stacked, (("space", 1),), 1)
    ksat_wide = widened[local_members]
    pressure = advance(widened[:local_members], ksat_wide, storage, recharge, own_counts)
    widened = padded_2(pressure, (("space", 1),), 1)
    pressure = advance(widened, ksat_wide, storage, recharge, own_counts)
    final_field = pressure.reshape(local_members, tile_cells)
    arrived = lax.all_to_all(final_field, "member", split_axis=0, concat_axis=0, tiled=True)
    by_owner = member_ids.reshape(groups, groups, share)
    arrived_ids = (
        jnp.take(by_owner, position, axis=1).reshape(local_members) - position * local_members
    )
    final_field = jnp.take(arrived, jnp.argsort(arrived_ids), axis=0)
    return final_field.reshape(local_members, tile_rows, tile_width)


def solution(mesh):
    return jax.shard_map(
        on_device,
        mesh=mesh,
        in_specs=(
            P("member", "space", None),
            P("space"),
            P("space"),
            P("space"),
            P("space", None),
            P("space", None),
            P("space", None),
            P(),
        ),
        out_specs=P("member", "space", None),
        check_vma=False,
    )
```

profile of v0, /device:TPU:8, one launch (start us, length us, event | category | flops | bytes accessed | tf_op | source)
XLA Modules:
  0.0 656.5 jit_solution(13870586919959672134)
XLA Ops:
  6.5 5.8 all_to_all.34
  12.4 6.6 %copy.22 = f32[64,4,4096]{2,0,1:T(8,128)} copy(f32[64,4,4096]{2,1,0:T(4,128)} %all_to_all.34) | data formatting | bytes 8388608 | tf_op jit(solution)/shard_map/all_to_all | solution.py:98
  19.0 5.0 all-to-all-start
  27.6 44.5 %all-to-all-done = f32[64,4,4096]{2,0,1:T(8,128)} async-done(((f32[64,4,4096]{2,0,1:T(8,128)}), f32[64,4,4096]{2,0,1:T(8,128)}, u32[]{:S(2)}, u32[]{:S(2)}) %all-to-all-start) | async-done | bytes 4194336 | tf_op jit(solution)/shard_map/all_to_all | solution.py:98
  74.6 6.2 gather_fusion.1
  80.7 4.8 bitcast_subtract_fusion
  85.5 5.6 copy.24
  91.1 5.7 gather_fusion
  100.8 39.6 %psum.15 = f32[256]{0:T(256)S(1)} all-reduce(f32[256]{0:T(256)S(1)} %bitcast.112), channel_id=1, replica_groups=mesh['member'=4,'space'=8] {'member','space'}, use_global_device_ids=true, to_apply=%region_5.6 | all-reduce | flops 256 | bytes 2048 | tf_op jit(solution)/shard_map/psum | solution.py:112
  140.4 86.6 %all-reduce.6.cloned.1.call-done = f32[256,256]{1,0:T(8,128)} async-done(((f32[256,256]{1,0:T(8,128)}), f32[256,256]{1,0:T(8,128)}) %all-reduce.6.cloned.1.call-update) | async-done | bytes 262160 | tf_op jit(solution)/shard_map/psum | solution.py:112
  247.0 8.2 %convolution_add_fusion = f32[256,4096]{1,0:T(8,128)} fusion(f32[256,4096]{1,0:T(8,128)} %bitcast_subtract_fusion, f32[4096]{0:T(1024)S(1)} %broadcast_multiply_fusion, f32[256,256]{1,0:T(8,128)S(1)} %gather_fusion.2, pred[256]{0:T(512)(128)(4,1)S(1)} %compare_and_fusion.1), kind=kOutput, calls=%fused_computation.51 | convolution fusion | flops 3222339584 | bytes 8667392 | tf_op jit(solution)/shard_map/dot_general | solution.py:128
  255.2 4.8 all-to-all-start.1
  262.5 45.8 %all-to-all-done.1 = f32[4,64,4096]{2,1,0:T(8,128)} async-done(((f32[4,64,4096]{2,1,0:T(8,128)}), f32[4,64,4096]{2,1,0:T(8,128)}, u32[]{:S(2)}, u32[]{:S(2)}) %all-to-all-start.1) | async-done | bytes 4194336 | tf_op jit(solution)/shard_map/all_to_all | solution.py:129
  308.3 6.9 %copy.28 = f32[64,4,4096]{2,1,0:T(4,128)} copy(f32[64,4,4096]{2,0,1:T(8,128)} %bitcast.13) | data formatting | bytes 8388608 | tf_op jit(solution)/shard_map/all_to_all | solution.py:129
  315.2 5.8 reshape.171
  321.0 3.6 pad_maximum_fusion.11
  324.6 3.4 collective-permute-start
  328.0 3.5 collective-permute-start.1
  331.5 3.3 fusion.69
  359.2 3.8 pad_maximum_fusion
  363.1 15.7 %fusion.6 = f32[64,16,1024]{2,1,0:T(8,128)} fusion(f32[64,18,1024]{2,1,0:T(8,128)S(1)} %get-tuple-element.768, f32[64,16,1024]{2,1,0:T(8,128)S(1)} %copy-done.2, f32[64,18,1024]{2,1,0:T(8,128)S(1)} %get-tuple-element.767, f32[65,1,1024]{2,1,0:T(1,128)} %collective-permute-done.1, f32[1,16,1024]{2,1,0:T(8,128)S(1)} %bitcast.106, ...), kind=kLoop, calls=%fused_computation.58 | loop fusion | flops 28311552 | bytes 34283520 | tf_op jit(solution)/shard_map/add | solution.py:70
  378.8 4.1 fusion.68
  382.9 6.3 while.168
  389.3 9.4 %while.167 = (s32[]{:T(128)}, f32[8,16,1024]{2,1,0:T(8,128)}, s32[]{:T(128)}, s32[8]{0:T(128)S(1)}, f32[16,1024]{1,0:T(8,128)S(1)}, /*index=5*/f32[8,16,1024]{2,1,0:T(8,128)}, s32[]{:T(128)}) while((s32[]{:T(128)}, f32[8,16,1024]{2,1,0:T(8,128)}, s32[]{:T(128)}, s32[8]{0:T(128)S(1)}, f32[16,1024]{1,0:T(8,128)S(1)}, ...), condition=%wide.region_26.27_spmd, body=%wide.region_25.26_spmd.sunk | while | flops 1441802 | bytes 1638537 | solution.py:66
  398.7 4.9 while.166
  403.6 6.9 %while.165 = (s32[]{:T(128)}, f32[8,16,1024]{2,1,0:T(8,128)S(1)}, s32[]{:T(128)}, s32[8]{0:T(128)S(1)}, f32[16,1024]{1,0:T(8,128)S(1)}, /*index=5*/f32[8,16,1024]{2,1,0:T(8,128)}, s32[]{:T(128)}) while((s32[]{:T(128)}, f32[8,16,1024]{2,1,0:T(8,128)S(1)}, s32[]{:T(128)}, s32[8]{0:T(128)S(1)}, f32[16,1024]{1,0:T(8,128)S(1)}, ...), condition=%wide.region_20.21_spmd, body=%wide.region_19.20_spmd.sunk | while | flops 1441802 | bytes 1638537 | solution.py:66
  410.5 7.2 %while.164 = (s32[]{:T(128)}, f32[8,16,1024]{2,1,0:T(8,128)S(1)}, s32[]{:T(128)}, s32[8]{0:T(128)S(1)}, f32[16,1024]{1,0:T(8,128)S(1)}, /*index=5*/f32[8,16,1024]{2,1,0:T(8,128)}, s32[]{:T(128)}) while((s32[]{:T(128)}, f32[8,16,1024]{2,1,0:T(8,128)S(1)}, s32[]{:T(128)}, s32[8]{0:T(128)S(1)}, f32[16,1024]{1,0:T(8,128)S(1)}, ...), condition=%wide.region_17.18_spmd, body=%wide.region_16.17_spmd.sunk | while | flops 1441802 | bytes 1638537 | solution.py:66
  417.7 16.9 %while.163 = (s32[]{:T(128)}, f32[8,16,1024]{2,1,0:T(8,128)S(1)}, s32[]{:T(128)}, s32[8]{0:T(128)S(1)}, f32[16,1024]{1,0:T(8,128)S(1)}, /*index=5*/f32[8,16,1024]{2,1,0:T(8,128)}, s32[]{:T(128)}) while((s32[]{:T(128)}, f32[8,16,1024]{2,1,0:T(8,128)S(1)}, s32[]{:T(128)}, s32[8]{0:T(128)S(1)}, f32[16,1024]{1,0:T(8,128)S(1)}, ...), condition=%wide.region_14.15_spmd, body=%wide.region_13.14_spmd.sunk | while | flops 1441802 | bytes 1638537 | solution.py:66
  434.6 4.6 while.162
  439.1 17.4 %while.161 = (s32[]{:T(128)}, f32[8,16,1024]{2,1,0:T(8,128)S(1)}, s32[]{:T(128)}, s32[8]{0:T(128)S(1)}, f32[16,1024]{1,0:T(8,128)S(1)}, /*index=5*/f32[8,16,1024]{2,1,0:T(8,128)}, s32[]{:T(128)}) while((s32[]{:T(128)}, f32[8,16,1024]{2,1,0:T(8,128)S(1)}, s32[]{:T(128)}, s32[8]{0:T(128)S(1)}, f32[16,1024]{1,0:T(8,128)S(1)}, ...), condition=%wide.region_8.9_spmd, body=%wide.region_7.8_spmd.sunk | while | flops 1441802 | bytes 1638537 | solution.py:66
  463.6 4.3 collective-permute-start.3
  467.9 6.3 collective-permute-done.2
  477.0 3.8 pad_maximum_fusion.3
  480.9 11.3 %fusion.18 = f32[64,16,1024]{2,1,0:T(8,128)} fusion(f32[64,18,1024]{2,1,0:T(8,128)S(1)} %get-tuple-element.770, f32[64,16,1024]{2,1,0:T(8,128)S(1)} %copy-done.8, f32[64,18,1024]{2,1,0:T(8,128)S(1)} %get-tuple-element.769, f32[64,1,1024]{2,1,0:T(1,128)} %collective-permute-done.3, f32[64,1,1024]{2,1,0:T(1,128)S(1)} %collective-permute-done.2, ...), kind=kLoop, calls=%fused_computation.70 | loop fusion | flops 26214400 | bytes 34209792 | tf_op jit(solution)/shard_map/add | solution.py:70
  492.2 4.1 fusion.66
  496.3 6.3 while.176
  502.7 9.4 %while.175 = (s32[]{:T(128)}, f32[8,16,1024]{2,1,0:T(8,128)}, s32[]{:T(128)}, s32[8]{0:T(128)S(1)}, f32[16,1024]{1,0:T(8,128)S(1)}, /*index=5*/f32[8,16,1024]{2,1,0:T(8,128)}, s32[]{:T(128)}) while((s32[]{:T(128)}, f32[8,16,1024]{2,1,0:T(8,128)}, s32[]{:T(128)}, s32[8]{0:T(128)S(1)}, f32[16,1024]{1,0:T(8,128)S(1)}, ...), condition=%wide.region_43.44_spmd, body=%wide.region_42.43_spmd.sunk | while | flops 1441802 | bytes 1638537 | solution.py:66
  512.0 4.9 while.174
  517.0 6.6 %while.173 = (s32[]{:T(128)}, f32[8,16,1024]{2,1,0:T(8,128)S(1)}, s32[]{:T(128)}, s32[8]{0:T(128)S(1)}, f32[16,1024]{1,0:T(8,128)S(1)}, /*index=5*/f32[8,16,1024]{2,1,0:T(8,128)}, s32[]{:T(128)}) while((s32[]{:T(128)}, f32[8,16,1024]{2,1,0:T(8,128)S(1)}, s32[]{:T(128)}, s32[8]{0:T(128)S(1)}, f32[16,1024]{1,0:T(8,128)S(1)}, ...), condition=%wide.region_39.40_spmd, body=%wide.region_38.39_spmd.sunk | while | flops 1441802 | bytes 1638537 | solution.py:66
  523.6 7.2 %while.172 = (s32[]{:T(128)}, f32[8,16,1024]{2,1,0:T(8,128)S(1)}, s32[]{:T(128)}, s32[8]{0:T(128)S(1)}, f32[16,1024]{1,0:T(8,128)S(1)}, /*index=5*/f32[8,16,1024]{2,1,0:T(8,128)}, s32[]{:T(128)}) while((s32[]{:T(128)}, f32[8,16,1024]{2,1,0:T(8,128)S(1)}, s32[]{:T(128)}, s32[8]{0:T(128)S(1)}, f32[16,1024]{1,0:T(8,128)S(1)}, ...), condition=%wide.region_37.38_spmd, body=%wide.region_36.37_spmd.sunk | while | flops 1441802 | bytes 1638537 | solution.py:66
  530.8 16.9 %while.171 = (s32[]{:T(128)}, f32[8,16,1024]{2,1,0:T(8,128)S(1)}, s32[]{:T(128)}, s32[8]{0:T(128)S(1)}, f32[16,1024]{1,0:T(8,128)S(1)}, /*index=5*/f32[8,16,1024]{2,1,0:T(8,128)}, s32[]{:T(128)}) while((s32[]{:T(128)}, f32[8,16,1024]{2,1,0:T(8,128)S(1)}, s32[]{:T(128)}, s32[8]{0:T(128)S(1)}, f32[16,1024]{1,0:T(8,128)S(1)}, ...), condition=%wide.region_35.36_spmd, body=%wide.region_34.35_spmd.sunk | while | flops 1441802 | bytes 1638537 | solution.py:66
  547.7 4.6 while.170
  552.3 17.4 %while.169 = (s32[]{:T(128)}, f32[8,16,1024]{2,1,0:T(8,128)S(1)}, s32[]{:T(128)}, s32[8]{0:T(128)S(1)}, f32[16,1024]{1,0:T(8,128)S(1)}, /*index=5*/f32[8,16,1024]{2,1,0:T(8,128)}, s32[]{:T(128)}) while((s32[]{:T(128)}, f32[8,16,1024]{2,1,0:T(8,128)S(1)}, s32[]{:T(128)}, s32[8]{0:T(128)S(1)}, f32[16,1024]{1,0:T(8,128)S(1)}, ...), condition=%wide.region_31.32_spmd, body=%wide.region_30.31_spmd.sunk | while | flops 1441802 | bytes 1638537 | solution.py:66
  576.3 5.0 all_to_all.41
  581.3 5.1 all-to-all-start.2
  589.3 45.2 %all-to-all-done.2 = f32[4,16,16384]{2,1,0:T(8,128)} async-done(((f32[4,16,16384]{2,1,0:T(8,128)}), f32[4,16,16384]{2,1,0:T(8,128)}, u32[]{:S(2)}, u32[]{:S(2)}) %all-to-all-start.2) | async-done | bytes 4194336 | tf_op jit(solution)/shard_map/all_to_all | solution.py:138
  634.6 7.7 %gather_fusion.4 = f32[64,16384]{1,0:T(8,128)} fusion(f32[64,16384]{1,0:T(8,128)} %bitcast.16, s32[1024]{0:T(1024)S(1)} %pad_clamp_fusion), kind=kCustom, calls=%fused_computation.4 | custom fusion | bytes 8388864 | tf_op jit(solution)/shard_map/jit(_take)/gather | solution.py:143
  642.3 4.6 copy.36
  (279 shorter events, 174.9 us)
Async XLA Ops:
  19.0 5.0 copy-start.1
  19.0 8.6 %copy-start.14 = (s32[1024]{0:T(1024)S(1)}, s32[1024]{0:T(1024)}, u32[]{:S(2)}) copy-start(s32[1024]{0:T(1024)} %param.41) | copy-start | bytes 12292
  19.0 53.2 %all-to-all-start = ((f32[64,4,4096]{2,0,1:T(8,128)}), f32[64,4,4096]{2,0,1:T(8,128)}, u32[]{:S(2)}, u32[]{:S(2)}) async-start(f32[64,4,4096]{2,0,1:T(8,128)} %copy.22), calls=%async_computation | async-start | bytes 8388608 | tf_op jit(solution)/shard_map/all_to_all | solution.py:98
  23.9 203.0 %all-reduce.6.cloned.1.call-start = ((), (), s32[]{:S(2)}) async-start(), calls=%async_computation.3 | async-start | bytes 524288 | tf_op jit(solution)/shard_map/psum | solution.py:112
  27.3 44.8 %copy-start.13 = (s32[4,16,4]{2,1,0:T(8,128)}, s32[4,16,4]{2,1,0:T(8,128)S(1)}, u32[]{:S(2)}) copy-start(s32[4,16,4]{2,1,0:T(8,128)S(1)} %reshape.168) | copy-start | bytes 3076
  91.1 5.7 copy-start.15
  91.1 5.7 copy-start.16
  255.2 53.0 %all-to-all-start.1 = ((f32[4,64,4096]{2,1,0:T(8,128)}), f32[4,64,4096]{2,1,0:T(8,128)}, u32[]{:S(2)}, u32[]{:S(2)}) async-start(f32[4,64,4096]{2,1,0:T(8,128)} %bitcast.102), calls=%async_computation.1 | async-start | bytes 8388608 | tf_op jit(solution)/shard_map/all_to_all | solution.py:129
  315.2 5.8 copy-start.9
  324.6 32.5 %collective-permute-start = (f32[65,1,1024]{2,1,0:T(1,128)}, f32[65,1,1024]{2,1,0:T(1,128)S(1)}, u32[]{:S(2)}, u32[]{:S(2)}) collective-permute-start(f32[65,1,1024]{2,1,0:T(1,128)} %get-tuple-element.771), channel_id=1, source_target_pairs={{0,1},{1,2},{2,3},{3,4},{4,5},{5,6},{6,7},{8,9},{9,10},{10,11},{11... | collective-permute-start | bytes 798728 | tf_op jit(solution)/shard_map/ppermute | solution.py:19
  328.0 29.1 %collective-permute-start.1 = (f32[65,1,1024]{2,1,0:T(1,128)}, f32[65,1,1024]{2,1,0:T(1,128)}, u32[]{:S(2)}, u32[]{:S(2)}) collective-permute-start(f32[65,1,1024]{2,1,0:T(1,128)} %get-tuple-element.772), channel_id=1, source_target_pairs={{1,0},{2,1},{3,2},{4,3},{5,4},{6,5},{7,6},{9,8},{10,9},{11,10},{12... | collective-permute-start | bytes 798728 | tf_op jit(solution)/shard_map/ppermute | solution.py:20
  357.0 2.2 copy-start.2
  359.2 3.8 copy-start.10
  359.2 3.8 copy-start
  359.2 3.8 copy-start.11
  378.8 4.1 copy-start.21
  382.9 6.4 copy-start.20
  389.2 9.4 %copy-start.19 = (s32[8]{0:T(128)S(1)}, s32[8]{0:T(128)}, u32[]{:S(2)}) copy-start(s32[8]{0:T(128)} %get-tuple-element.1693) | copy-start | bytes 100
  398.6 5.0 copy-start.18
  403.6 6.9 %copy-start.17 = (s32[8]{0:T(128)S(1)}, s32[8]{0:T(128)}, u32[]{:S(2)}) copy-start(s32[8]{0:T(128)} %get-tuple-element.1651) | copy-start | bytes 100
  456.5 1.0 copy-start.3
  456.6 1.2 copy-start.5
  457.8 2.0 copy-start.7
  461.1 13.1 %collective-permute-start.2 = (f32[64,1,1024]{2,1,0:T(1,128)}, f32[64,1,1024]{2,1,0:T(1,128)S(1)}, u32[]{:S(2)}, u32[]{:S(2)}) collective-permute-start(f32[64,1,1024]{2,1,0:T(1,128)} %get-tuple-element.781), channel_id=1, source_target_pairs={{0,1},{1,2},{2,3},{3,4},{4,5},{5,6},{6,7},{8,9},{9,10},{10,11},{11... | collective-permute-start | bytes 786440 | tf_op jit(solution)/shard_map/ppermute | solution.py:19
  463.6 13.4 %collective-permute-start.3 = (f32[64,1,1024]{2,1,0:T(1,128)}, f32[64,1,1024]{2,1,0:T(1,128)}, u32[]{:S(2)}, u32[]{:S(2)}) collective-permute-start(f32[64,1,1024]{2,1,0:T(1,128)} %get-tuple-element.782), channel_id=1, source_target_pairs={{1,0},{2,1},{3,2},{4,3},{5,4},{6,5},{7,6},{9,8},{10,9},{11,10},{12... | collective-permute-start | bytes 786440 | tf_op jit(solution)/shard_map/ppermute | solution.py:20
  467.9 13.0 %copy-start.8 = (f32[64,16,1024]{2,1,0:T(8,128)S(1)}, f32[64,16,1024]{2,1,0:T(8,128)}, u32[]{:S(2)}) copy-start(f32[64,16,1024]{2,1,0:T(8,128)} %copy-done.7) | copy-start | bytes 12582916
  467.9 13.0 %copy-start.12 = (f32[16,1024]{1,0:T(8,128)S(1)}, f32[16,1024]{1,0:T(8,128)}, u32[]{:S(2)}) copy-start(f32[16,1024]{1,0:T(8,128)} %param.46) | copy-start | bytes 196612
  569.7 5.0 copy-start.4
  569.7 5.8 copy-start.6
  581.3 53.3 %all-to-all-start.2 = ((f32[4,16,16384]{2,1,0:T(8,128)}), f32[4,16,16384]{2,1,0:T(8,128)}, u32[]{:S(2)}, u32[]{:S(2)}) async-start(f32[4,16,16384]{2,1,0:T(8,128)} %all_to_all.41), calls=%async_computation.2 | async-start | bytes 8388608 | tf_op jit(solution)/shard_map/all_to_all | solution.py:138
Sparse Core Ops, SparseCore 0:
  100.1 126.7 all-reduce.5
where the time goes:
time: 669 us; the launch traced here: 656 us
  waiting for transfers between devices  231 us (35%)
  other arithmetic  155 us (23%)
  local copies, waits for them, and re-layouts  109 us (16%)
  loops' own time  49.4 us (7%)
  blocking collectives  39.6 us (6%)
  starting transfers between devices  28.5 us (4%)
  matrix products  28.2 us (4%)
  between operations  15.5 us (2%)
    select_n x62, other arithmetic, sweep_once(): jnp.where((group_counts > sweep_index)[:, None, None], stepped, iterate)  97 us
    psum x1, waiting for transfers between devices, on_device(): lax.psum((gram_part, drive_part), ('member', 'space'))  86.6 us
    another operation x16, loops' own time, sweep_group(): return lax.fori_loop(0, jnp.max(group_counts), sweep_once, start_iter)  49.4 us
    all_to_all x1, waiting for transfers between devices, on_device(): lax.all_to_all(analysis, 'member', split_axis=0, concat_axis=1, tiled=True)  45.8 us
    all_to_all x1, waiting for transfers between devices, on_device(): lax.all_to_all(final_field, 'member', split_axis=0, concat_axis=0, tiled=...  45.2 us
    all_to_all x1, waiting for transfers between devices, on_device(): lax.all_to_all(state.reshape(local_members, tile_cells), 'member', split_...  44.5 us
    psum x1, blocking collectives, on_device(): lax.psum((gram_part, drive_part), ('member', 'space'))  39.6 us
    add x2, other arithmetic, relax(): target = pressure + storage * jnp.tanh(pressure) + drive_term  27 us
  transfers between devices with their start and end apart: 8, of which 6 were waited for; matrix products, arithmetic and copies ran while one was open for 5% of the time, Pallas kernels for 0%

commit v1 on v0

--- a/solution.py
+++ b/solution.py
@@ -109,7 +109,7 @@
     innovation = weight * (obs_value - jnp.take(mean_state, picked))
     gram_part = jnp.dot(spread, spread.T, precision=HIGHEST_PRECISION)
     drive_part = jnp.dot(spread, innovation, precision=HIGHEST_PRECISION)
-    gram_matrix, drive_vector = lax.psum((gram_part, drive_part), ("member", "space"))
+    gram_matrix, drive_vector = lax.psum(lax.psum((gram_part, drive_part), "space"), "member")
     root_inverse = inverse_root(gram_matrix)
     mean_weights = jnp.dot(
         root_inverse,

time: 669 us -> 646 us (0.966)
  blocking collectives: 39.6 us -> 23.2 us
    psum x1 -> x2, blocking collectives: 39.6 us -> 23.2 us  [the longest x1 17.4 us: on_device(): lax.psum((gram_part, drive_part), 'space')]
    psum x1 -> x2, waiting for transfers between devices: 86.6 us -> 81 us  [the longest x1 70.7 us: on_device(): lax.psum((gram_part, drive_part), 'space')]
  transfers between devices with their start and end apart: 8 -> 9, of which waited for: 6 -> 7; matrix products, arithmetic and copies ran while one was open for 5% -> 6% of each run, Pallas kernels for 0% -> 0%
where the time goes in v1:
time: 646 us; the launch traced here: 635 us
  waiting for transfers between devices  226 us (35%)
  other arithmetic  155 us (24%)
  local copies, waits for them, and re-layouts  109 us (17%)
  loops' own time  49.4 us (8%)
  starting transfers between devices  28.6 us (4%)
  matrix products  28.2 us (4%)
  blocking collectives  23.2 us (4%)
  between operations  15.5 us (2%)
    select_n x62, other arithmetic, sweep_once(): jnp.where((group_counts > sweep_index)[:, None, None], stepped, iterate)  97 us
    psum x1, waiting for transfers between devices, on_device(): lax.psum((gram_part, drive_part), 'space')  70.7 us
    another operation x16, loops' own time, sweep_group(): return lax.fori_loop(0, jnp.max(group_counts), sweep_once, start_iter)  49.4 us
    all_to_all x1, waiting for transfers between devices, on_device(): lax.all_to_all(analysis, 'member', split_axis=0, concat_axis=1, tiled=True)  45.7 us
    all_to_all x1, waiting for transfers between devices, on_device(): lax.all_to_all(final_field, 'member', split_axis=0, concat_axis=0, tiled=...  45.2 us
    all_to_all x1, waiting for transfers between devices, on_device(): lax.all_to_all(state.reshape(local_members, tile_cells), 'member', split_...  44.6 us
    add x2, other arithmetic, relax(): target = pressure + storage * jnp.tanh(pressure) + drive_term  27 us
    slice x17, local copies, waits for them, and re-layouts, relax(): pressure[first_member:first_member + 8]  25.5 us
  transfers between devices with their start and end apart: 9, of which 7 were waited for; matrix products, arithmetic and copies ran while one was open for 6% of the time, Pallas kernels for 0%

profile of v1, /device:TPU:8, one launch (start us, length us, event | category | flops | bytes accessed | tf_op | source)
XLA Modules:
  0.0 634.7 jit_solution(17171072031008341010)
XLA Ops:
  6.5 5.8 all_to_all.34
  12.4 6.6 %copy.22 = f32[64,4,4096]{2,0,1:T(8,128)} copy(f32[64,4,4096]{2,1,0:T(4,128)} %all_to_all.34) | data formatting | bytes 8388608 | tf_op jit(solution)/shard_map/all_to_all | solution.py:98
  19.0 5.0 all-to-all-start
  27.5 44.6 %all-to-all-done = f32[64,4,4096]{2,0,1:T(8,128)} async-done(((f32[64,4,4096]{2,0,1:T(8,128)}), f32[64,4,4096]{2,0,1:T(8,128)}, u32[]{:S(2)}, u32[]{:S(2)}) %all-to-all-start) | async-done | bytes 4194336 | tf_op jit(solution)/shard_map/all_to_all | solution.py:98
  74.6 6.2 gather_fusion.1
  80.7 4.8 bitcast_subtract_fusion
  85.5 5.6 copy.24
  91.1 5.7 gather_fusion
  100.1 70.7 %all-reduce.7.cloned.1.call-done = f32[256,256]{1,0:T(8,128)} async-done(((f32[256,256]{1,0:T(8,128)}), f32[256,256]{1,0:T(8,128)}) %all-reduce.7.cloned.1.call-update) | async-done | bytes 262160 | tf_op jit(solution)/shard_map/psum | solution.py:112
  171.7 17.4 %psum.30 = f32[256]{0:T(256)S(1)} all-reduce(f32[256]{0:T(256)S(1)} %bitcast.112), channel_id=1, replica_groups=mesh['member'=4,'space'=8] {'space'}, use_global_device_ids=true, to_apply=%region_6.7 | all-reduce | flops 256 | bytes 2048 | tf_op jit(solution)/shard_map/psum | solution.py:112
  189.1 5.8 psum.31
  194.9 10.3 %all-reduce.9.cloned.1.call-done = f32[256,256]{1,0:T(8,128)} async-done(((f32[256,256]{1,0:T(8,128)}), f32[256,256]{1,0:T(8,128)}) %all-reduce.9.cloned.1.call-update) | async-done | bytes 262160 | tf_op jit(solution)/shard_map/psum | solution.py:112
  225.2 8.2 %convolution_add_fusion = f32[256,4096]{1,0:T(8,128)} fusion(f32[256,4096]{1,0:T(8,128)} %bitcast_subtract_fusion, f32[4096]{0:T(1024)S(1)} %broadcast_multiply_fusion, f32[256,256]{1,0:T(8,128)S(1)} %gather_fusion.2, pred[256]{0:T(512)(128)(4,1)S(1)} %compare_and_fusion.1), kind=kOutput, calls=%fused_computation.51 | convolution fusion | flops 3222339584 | bytes 8667392 | tf_op jit(solution)/shard_map/dot_general | solution.py:128
  233.4 4.8 all-to-all-start.1
  240.7 45.7 %all-to-all-done.1 = f32[4,64,4096]{2,1,0:T(8,128)} async-done(((f32[4,64,4096]{2,1,0:T(8,128)}), f32[4,64,4096]{2,1,0:T(8,128)}, u32[]{:S(2)}, u32[]{:S(2)}) %all-to-all-start.1) | async-done | bytes 4194336 | tf_op jit(solution)/shard_map/all_to_all | solution.py:129
  286.4 6.9 %copy.28 = f32[64,4,4096]{2,1,0:T(4,128)} copy(f32[64,4,4096]{2,0,1:T(8,128)} %bitcast.13) | data formatting | bytes 8388608 | tf_op jit(solution)/shard_map/all_to_all | solution.py:129
  293.3 5.8 reshape.171
  299.2 3.6 pad_maximum_fusion.11
  306.1 3.5 collective-permute-start.1
  337.4 3.8 pad_maximum_fusion
  341.2 15.7 %fusion.6 = f32[64,16,1024]{2,1,0:T(8,128)} fusion(f32[64,18,1024]{2,1,0:T(8,128)S(1)} %get-tuple-element.768, f32[64,16,1024]{2,1,0:T(8,128)S(1)} %copy-done.2, f32[64,18,1024]{2,1,0:T(8,128)S(1)} %get-tuple-element.767, f32[65,1,1024]{2,1,0:T(1,128)} %collective-permute-done.1, f32[1,16,1024]{2,1,0:T(8,128)S(1)} %bitcast.106, ...), kind=kLoop, calls=%fused_computation.58 | loop fusion | flops 28311552 | bytes 34283520 | tf_op jit(solution)/shard_map/add | solution.py:70
  356.9 4.2 fusion.68
  361.1 6.3 while.168
  367.4 9.6 %while.167 = (s32[]{:T(128)}, f32[8,16,1024]{2,1,0:T(8,128)}, s32[]{:T(128)}, s32[8]{0:T(128)S(1)}, f32[16,1024]{1,0:T(8,128)S(1)}, /*index=5*/f32[8,16,1024]{2,1,0:T(8,128)}, s32[]{:T(128)}) while((s32[]{:T(128)}, f32[8,16,1024]{2,1,0:T(8,128)}, s32[]{:T(128)}, s32[8]{0:T(128)S(1)}, f32[16,1024]{1,0:T(8,128)S(1)}, ...), condition=%wide.region_28.29_spmd, body=%wide.region_27.28_spmd.sunk | while | flops 1441802 | bytes 1638537 | solution.py:66
  377.1 4.7 while.166
  381.8 6.8 %while.165 = (s32[]{:T(128)}, f32[8,16,1024]{2,1,0:T(8,128)S(1)}, s32[]{:T(128)}, s32[8]{0:T(128)S(1)}, f32[16,1024]{1,0:T(8,128)S(1)}, /*index=5*/f32[8,16,1024]{2,1,0:T(8,128)}, s32[]{:T(128)}) while((s32[]{:T(128)}, f32[8,16,1024]{2,1,0:T(8,128)S(1)}, s32[]{:T(128)}, s32[8]{0:T(128)S(1)}, f32[16,1024]{1,0:T(8,128)S(1)}, ...), condition=%wide.region_22.23_spmd, body=%wide.region_21.22_spmd.sunk | while | flops 1441802 | bytes 1638537 | solution.py:66
  388.6 6.9 %while.164 = (s32[]{:T(128)}, f32[8,16,1024]{2,1,0:T(8,128)S(1)}, s32[]{:T(128)}, s32[8]{0:T(128)S(1)}, f32[16,1024]{1,0:T(8,128)S(1)}, /*index=5*/f32[8,16,1024]{2,1,0:T(8,128)}, s32[]{:T(128)}) while((s32[]{:T(128)}, f32[8,16,1024]{2,1,0:T(8,128)S(1)}, s32[]{:T(128)}, s32[8]{0:T(128)S(1)}, f32[16,1024]{1,0:T(8,128)S(1)}, ...), condition=%wide.region_19.20_spmd, body=%wide.region_18.19_spmd.sunk | while | flops 1441802 | bytes 1638537 | solution.py:66
  395.5 17.3 %while.163 = (s32[]{:T(128)}, f32[8,16,1024]{2,1,0:T(8,128)S(1)}, s32[]{:T(128)}, s32[8]{0:T(128)S(1)}, f32[16,1024]{1,0:T(8,128)S(1)}, /*index=5*/f32[8,16,1024]{2,1,0:T(8,128)}, s32[]{:T(128)}) while((s32[]{:T(128)}, f32[8,16,1024]{2,1,0:T(8,128)S(1)}, s32[]{:T(128)}, s32[8]{0:T(128)S(1)}, f32[16,1024]{1,0:T(8,128)S(1)}, ...), condition=%wide.region_16.17_spmd, body=%wide.region_15.16_spmd.sunk | while | flops 1441802 | bytes 1638537 | solution.py:66
  412.8 5.0 while.162
  417.8 16.9 %while.161 = (s32[]{:T(128)}, f32[8,16,1024]{2,1,0:T(8,128)S(1)}, s32[]{:T(128)}, s32[8]{0:T(128)S(1)}, f32[16,1024]{1,0:T(8,128)S(1)}, /*index=5*/f32[8,16,1024]{2,1,0:T(8,128)}, s32[]{:T(128)}) while((s32[]{:T(128)}, f32[8,16,1024]{2,1,0:T(8,128)S(1)}, s32[]{:T(128)}, s32[8]{0:T(128)S(1)}, f32[16,1024]{1,0:T(8,128)S(1)}, ...), condition=%wide.region_10.11_spmd, body=%wide.region_9.10_spmd.sunk | while | flops 1441802 | bytes 1638537 | solution.py:66
  441.8 4.3 collective-permute-start.3
  446.1 6.4 %collective-permute-done.2 = f32[64,1,1024]{2,1,0:T(1,128)S(1)} collective-permute-done((f32[64,1,1024]{2,1,0:T(1,128)}, f32[64,1,1024]{2,1,0:T(1,128)S(1)}, u32[]{:S(2)}, u32[]{:S(2)}) %collective-permute-start.2) | collective-permute-done | bytes 262176 | tf_op jit(solution)/shard_map/ppermute | solution.py:19
  455.2 3.8 pad_maximum_fusion.3
  459.1 11.3 %fusion.18 = f32[64,16,1024]{2,1,0:T(8,128)} fusion(f32[64,18,1024]{2,1,0:T(8,128)S(1)} %get-tuple-element.770, f32[64,16,1024]{2,1,0:T(8,128)S(1)} %copy-done.8, f32[64,18,1024]{2,1,0:T(8,128)S(1)} %get-tuple-element.769, f32[64,1,1024]{2,1,0:T(1,128)} %collective-permute-done.3, f32[64,1,1024]{2,1,0:T(1,128)S(1)} %collective-permute-done.2, ...), kind=kLoop, calls=%fused_computation.70 | loop fusion | flops 26214400 | bytes 34209792 | tf_op jit(solution)/shard_map/add | solution.py:70
  470.4 4.2 fusion.66
  474.5 6.3 while.176
  480.9 9.6 %while.175 = (s32[]{:T(128)}, f32[8,16,1024]{2,1,0:T(8,128)}, s32[]{:T(128)}, s32[8]{0:T(128)S(1)}, f32[16,1024]{1,0:T(8,128)S(1)}, /*index=5*/f32[8,16,1024]{2,1,0:T(8,128)}, s32[]{:T(128)}) while((s32[]{:T(128)}, f32[8,16,1024]{2,1,0:T(8,128)}, s32[]{:T(128)}, s32[8]{0:T(128)S(1)}, f32[16,1024]{1,0:T(8,128)S(1)}, ...), condition=%wide.region_45.46_spmd, body=%wide.region_44.45_spmd.sunk | while | flops 1441802 | bytes 1638537 | solution.py:66
  490.5 4.7 while.174
  495.1 6.6 %while.173 = (s32[]{:T(128)}, f32[8,16,1024]{2,1,0:T(8,128)S(1)}, s32[]{:T(128)}, s32[8]{0:T(128)S(1)}, f32[16,1024]{1,0:T(8,128)S(1)}, /*index=5*/f32[8,16,1024]{2,1,0:T(8,128)}, s32[]{:T(128)}) while((s32[]{:T(128)}, f32[8,16,1024]{2,1,0:T(8,128)S(1)}, s32[]{:T(128)}, s32[8]{0:T(128)S(1)}, f32[16,1024]{1,0:T(8,128)S(1)}, ...), condition=%wide.region_41.42_spmd, body=%wide.region_40.41_spmd.sunk | while | flops 1441802 | bytes 1638537 | solution.py:66
  501.7 6.9 %while.172 = (s32[]{:T(128)}, f32[8,16,1024]{2,1,0:T(8,128)S(1)}, s32[]{:T(128)}, s32[8]{0:T(128)S(1)}, f32[16,1024]{1,0:T(8,128)S(1)}, /*index=5*/f32[8,16,1024]{2,1,0:T(8,128)}, s32[]{:T(128)}) while((s32[]{:T(128)}, f32[8,16,1024]{2,1,0:T(8,128)S(1)}, s32[]{:T(128)}, s32[8]{0:T(128)S(1)}, f32[16,1024]{1,0:T(8,128)S(1)}, ...), condition=%wide.region_39.40_spmd, body=%wide.region_38.39_spmd.sunk | while | flops 1441802 | bytes 1638537 | solution.py:66
  508.7 17.3 %while.171 = (s32[]{:T(128)}, f32[8,16,1024]{2,1,0:T(8,128)S(1)}, s32[]{:T(128)}, s32[8]{0:T(128)S(1)}, f32[16,1024]{1,0:T(8,128)S(1)}, /*index=5*/f32[8,16,1024]{2,1,0:T(8,128)}, s32[]{:T(128)}) while((s32[]{:T(128)}, f32[8,16,1024]{2,1,0:T(8,128)S(1)}, s32[]{:T(128)}, s32[8]{0:T(128)S(1)}, f32[16,1024]{1,0:T(8,128)S(1)}, ...), condition=%wide.region_37.38_spmd, body=%wide.region_36.37_spmd.sunk | while | flops 1441802 | bytes 1638537 | solution.py:66
  526.0 5.0 while.170
  531.0 16.9 %while.169 = (s32[]{:T(128)}, f32[8,16,1024]{2,1,0:T(8,128)S(1)}, s32[]{:T(128)}, s32[8]{0:T(128)S(1)}, f32[16,1024]{1,0:T(8,128)S(1)}, /*index=5*/f32[8,16,1024]{2,1,0:T(8,128)}, s32[]{:T(128)}) while((s32[]{:T(128)}, f32[8,16,1024]{2,1,0:T(8,128)S(1)}, s32[]{:T(128)}, s32[8]{0:T(128)S(1)}, f32[16,1024]{1,0:T(8,128)S(1)}, ...), condition=%wide.region_33.34_spmd, body=%wide.region_32.33_spmd.sunk | while | flops 1441802 | bytes 1638537 | solution.py:66
  554.5 5.0 all_to_all.41
  559.5 5.1 all-to-all-start.2
  567.5 45.2 %all-to-all-done.2 = f32[4,16,16384]{2,1,0:T(8,128)} async-done(((f32[4,16,16384]{2,1,0:T(8,128)}), f32[4,16,16384]{2,1,0:T(8,128)}, u32[]{:S(2)}, u32[]{:S(2)}) %all-to-all-start.2) | async-done | bytes 4194336 | tf_op jit(solution)/shard_map/all_to_all | solution.py:138
  612.8 7.7 %gather_fusion.4 = f32[64,16384]{1,0:T(8,128)} fusion(f32[64,16384]{1,0:T(8,128)} %bitcast.16, s32[1024]{0:T(1024)S(1)} %pad_clamp_fusion), kind=kCustom, calls=%fused_computation.4 | custom fusion | bytes 8388864 | tf_op jit(solution)/shard_map/jit(_take)/gather | solution.py:143
  620.5 4.6 copy.36
  (283 shorter events, 181.6 us)
Async XLA Ops:
  19.0 5.0 copy-start.1
  19.0 8.5 %copy-start.14 = (s32[1024]{0:T(1024)S(1)}, s32[1024]{0:T(1024)}, u32[]{:S(2)}) copy-start(s32[1024]{0:T(1024)} %param.41) | copy-start | bytes 12292
  19.0 53.2 %all-to-all-start = ((f32[64,4,4096]{2,0,1:T(8,128)}), f32[64,4,4096]{2,0,1:T(8,128)}, u32[]{:S(2)}, u32[]{:S(2)}) async-start(f32[64,4,4096]{2,0,1:T(8,128)} %copy.22), calls=%async_computation | async-start | bytes 8388608 | tf_op jit(solution)/shard_map/all_to_all | solution.py:98
  23.9 146.9 %all-reduce.7.cloned.1.call-start = ((), (), s32[]{:S(2)}) async-start(), calls=%async_computation.3 | async-start | bytes 524288 | tf_op jit(solution)/shard_map/psum | solution.py:112
  27.3 44.8 %copy-start.13 = (s32[4,16,4]{2,1,0:T(8,128)}, s32[4,16,4]{2,1,0:T(8,128)S(1)}, u32[]{:S(2)}) copy-start(s32[4,16,4]{2,1,0:T(8,128)S(1)} %reshape.168) | copy-start | bytes 3076
  91.1 5.7 copy-start.15
  91.1 5.7 copy-start.16
  100.0 105.2 %all-reduce.9.cloned.1.call-start = ((), (), s32[]{:S(2)}) async-start(), calls=%async_computation.4 | async-start | bytes 524288 | tf_op jit(solution)/shard_map/psum | solution.py:112
  233.4 53.0 %all-to-all-start.1 = ((f32[4,64,4096]{2,1,0:T(8,128)}), f32[4,64,4096]{2,1,0:T(8,128)}, u32[]{:S(2)}, u32[]{:S(2)}) async-start(f32[4,64,4096]{2,1,0:T(8,128)} %bitcast.102), calls=%async_computation.1 | async-start | bytes 8388608 | tf_op jit(solution)/shard_map/all_to_all | solution.py:129
  293.3 5.8 copy-start.9
  302.8 32.5 %collective-permute-start = (f32[65,1,1024]{2,1,0:T(1,128)}, f32[65,1,1024]{2,1,0:T(1,128)S(1)}, u32[]{:S(2)}, u32[]{:S(2)}) collective-permute-start(f32[65,1,1024]{2,1,0:T(1,128)} %get-tuple-element.771), channel_id=1, source_target_pairs={{0,1},{1,2},{2,3},{3,4},{4,5},{5,6},{6,7},{8,9},{9,10},{10,11},{11... | collective-permute-start | bytes 798728 | tf_op jit(solution)/shard_map/ppermute | solution.py:19
  306.1 29.1 %collective-permute-start.1 = (f32[65,1,1024]{2,1,0:T(1,128)}, f32[65,1,1024]{2,1,0:T(1,128)}, u32[]{:S(2)}, u32[]{:S(2)}) collective-permute-start(f32[65,1,1024]{2,1,0:T(1,128)} %get-tuple-element.772), channel_id=1, source_target_pairs={{1,0},{2,1},{3,2},{4,3},{5,4},{6,5},{7,6},{9,8},{10,9},{11,10},{12... | collective-permute-start | bytes 798728 | tf_op jit(solution)/shard_map/ppermute | solution.py:20
  335.2 2.2 copy-start.2
  337.4 3.8 copy-start.10
  337.4 3.8 copy-start
  337.4 3.8 copy-start.11
  356.9 4.2 copy-start.21
  361.1 6.4 %copy-start.20 = (s32[8]{0:T(128)S(1)}, s32[8]{0:T(128)}, u32[]{:S(2)}) copy-start(s32[8]{0:T(128)} %get-tuple-element.1714) | copy-start | bytes 100
  367.4 9.7 %copy-start.19 = (s32[8]{0:T(128)S(1)}, s32[8]{0:T(128)}, u32[]{:S(2)}) copy-start(s32[8]{0:T(128)} %get-tuple-element.1693) | copy-start | bytes 100
  377.1 4.7 copy-start.18
  381.7 6.8 %copy-start.17 = (s32[8]{0:T(128)S(1)}, s32[8]{0:T(128)}, u32[]{:S(2)}) copy-start(s32[8]{0:T(128)} %get-tuple-element.1651) | copy-start | bytes 100
  434.7 1.0 copy-start.3
  434.7 1.2 copy-start.5
  436.0 2.0 copy-start.7
  439.3 13.1 %collective-permute-start.2 = (f32[64,1,1024]{2,1,0:T(1,128)}, f32[64,1,1024]{2,1,0:T(1,128)S(1)}, u32[]{:S(2)}, u32[]{:S(2)}) collective-permute-start(f32[64,1,1024]{2,1,0:T(1,128)} %get-tuple-element.781), channel_id=1, source_target_pairs={{0,1},{1,2},{2,3},{3,4},{4,5},{5,6},{6,7},{8,9},{9,10},{10,11},{11... | collective-permute-start | bytes 786440 | tf_op jit(solution)/shard_map/ppermute | solution.py:19
  441.8 13.4 %collective-permute-start.3 = (f32[64,1,1024]{2,1,0:T(1,128)}, f32[64,1,1024]{2,1,0:T(1,128)}, u32[]{:S(2)}, u32[]{:S(2)}) collective-permute-start(f32[64,1,1024]{2,1,0:T(1,128)} %get-tuple-element.782), channel_id=1, source_target_pairs={{1,0},{2,1},{3,2},{4,3},{5,4},{6,5},{7,6},{9,8},{10,9},{11,10},{12... | collective-permute-start | bytes 786440 | tf_op jit(solution)/shard_map/ppermute | solution.py:20
  446.1 13.0 %copy-start.8 = (f32[64,16,1024]{2,1,0:T(8,128)S(1)}, f32[64,16,1024]{2,1,0:T(8,128)}, u32[]{:S(2)}) copy-start(f32[64,16,1024]{2,1,0:T(8,128)} %copy-done.7) | copy-start | bytes 12582916
  446.1 13.0 %copy-start.12 = (f32[16,1024]{1,0:T(8,128)S(1)}, f32[16,1024]{1,0:T(8,128)}, u32[]{:S(2)}) copy-start(f32[16,1024]{1,0:T(8,128)} %param.46) | copy-start | bytes 196612
  547.9 5.0 copy-start.4
  547.9 5.8 copy-start.6
  559.5 53.3 %all-to-all-start.2 = ((f32[4,16,16384]{2,1,0:T(8,128)}), f32[4,16,16384]{2,1,0:T(8,128)}, u32[]{:S(2)}, u32[]{:S(2)}) async-start(f32[4,16,16384]{2,1,0:T(8,128)} %all_to_all.41), calls=%async_computation.2 | async-start | bytes 8388608 | tf_op jit(solution)/shard_map/all_to_all | solution.py:138
Sparse Core Ops, SparseCore 0:
  100.1 70.7 all-reduce.6
  173.2 31.9 all-reduce.8
